TPU v7x, 32 devices: a 4x4x1 block of a 4x4x8 slice. The times are simulated.
32 devices in a mesh: batch: 1 (over z), col: 4 (over y), row: 8 (over x, core).
Axes of the slice: x: 4, y: 4, z: 1, core: 2. Of those that a mesh axis runs over, the one named last changes fastest.
The devices are a block of a 4x4x8 slice.
Arguments:
- x: bfloat16 [16, 768, 32, 128], P('batch', 'row', 'col')
- w_down_1: bfloat16 [3, 3, 128, 256], replicated
- b_down_1: float32 [256], replicated
- w_conv_1: bfloat16 [3, 3, 256, 256], replicated
- b_conv_1: float32 [256], replicated
- w_proj_1: bfloat16 [128, 256], replicated
- w_down_2: bfloat16 [3, 3, 256, 320], replicated
- b_down_2: float32 [320], replicated
- w_conv_2: bfloat16 [3, 3, 320, 320], replicated
- b_conv_2: float32 [320], replicated
- w_proj_2: bfloat16 [256, 320], replicated
- w_down_3: bfloat16 [3, 3, 320, 320], replicated
- b_down_3: float32 [320], replicated
- w_conv_3: bfloat16 [3, 3, 320, 320], replicated
- b_conv_3: float32 [320], replicated
- w_proj_3: bfloat16 [320, 320], replicated
Outputs:
- output: bfloat16 [16, 96, 4, 320], P('batch', 'row', 'col')
All inputs are finite; a program needn't handle non-finite values.
Results may differ from a plain program's by a relative error of at most 0.00483591.
Values are sent between devices in bfloat16 or wider.
A program may use at most 768 MiB of HBM per device.

v0:
```python
import functools

import jax
import jax.numpy as jnp
from jax import lax
from jax.experimental import pallas as pl
from jax.experimental.pallas import tpu as pltpu
from jax.sharding import PartitionSpec as P

LANE = 128
MESH = pl.DeviceIdType.MESH
NEIGHBOURS = [(dr, dc) for dr in (-1, 0, 1) for dc in (-1, 0, 1) if (dr, dc) != (0, 0)]


def tiles_of(channels):
    return -(-channels // LANE)


def cut(count, pieces, unit=1):
    bounds = [round(count * k / pieces / unit) * unit for k in range(pieces + 1)]
    return [(a, b) for a, b in zip(bounds, bounds[1:]) if b > a]


class Exchange:
    def __init__(self, grid, sems, counter):
        self.grid, self.sems, self.counter = grid, sems, counter
        self.copies = {}
        self.waited = set()

    def exists(self, dr, dc):
        row, col, row_count, col_count = self.grid
        tests = []
        if dr == 1:
            tests.append(row + 1 < row_count)
        if dr == -1:
            tests.append(row > 0)
        if dc == 1:
            tests.append(col + 1 < col_count)
        if dc == -1:
            tests.append(col > 0)
        return functools.reduce(jnp.logical_and, tests)

    def send(self, key, dr, dc, src, dst):
        row, col = self.grid[:2]
        index = self.counter[0]
        self.counter[0] += 1
        copy = pltpu.make_async_remote_copy(
            src_ref=src, dst_ref=dst, send_sem=self.sems.at[0, index], recv_sem=self.sems.at[1, index],
            device_id={"row": row + dr, "col": col + dc}, device_id_type=MESH)
        self.copies[key] = (copy, dr, dc)
        pl.when(self.exists(dr, dc))(copy.start)

    def need(self, *keys):
        for key in keys:
            if key not in self.waited:
                self.waited.add(key)
                copy, dr, dc = self.copies[key]
                pl.when(self.exists(-dr, -dc))(copy.wait_recv)

    def finish(self):
        assert self.waited == set(self.copies)
        for copy, dr, dc in self.copies.values():
            pl.when(self.exists(dr, dc))(copy.wait_send)


def body(cfg, x_hbm, *refs):
    params, refs = refs[:15], refs[15:]
    out_ref, xs, ys, zs, ws, load_sems, sems = refs[0], refs[1], refs[2:5], refs[5:7], refs[7:16], refs[16], refs[17]
    chans, height, width = cfg["chans"], cfg["height"], cfg["width"]
    row, col = lax.axis_index("row"), lax.axis_index("col")
    grid = (row, col, cfg["rows"], cfg["cols"])
    counter = [0]
    dtype = jnp.bfloat16
    images = cfg["images"]

    loads = [pltpu.make_async_copy(x_hbm, xs.at[0, 1:, :, 1:], load_sems.at[0])]
    for stage in range(3):
        for k, p in enumerate((0, 2, 4)):
            src, dst = params[5 * stage + p], ws[3 * stage + k]
            if dst.shape != src.shape:
                dst = dst.at[:, :src.shape[1]]
            loads.append(pltpu.make_async_copy(src, dst, load_sems.at[1 + 3 * stage + k]))
    for load in loads[:4]:
        load.start()

    def zero(ref):
        ref[...] = jnp.zeros(ref.shape, ref.dtype)

    for buf in (xs,) + tuple(zs):
        zero(buf.at[:, 0, 1])
        zero(buf.at[:, :, :, 0, 1])
    for buf in ys:
        zero(buf.at[:, 0:1])
        zero(buf.at[:, -1:])
        zero(buf.at[:, :, 0:1])
        zero(buf.at[:, :, -1:])
    for buf in tuple(ys[1:]) + tuple(zs[1:]):
        zero(buf.at[buf.shape[0] - 1:])
    for k, p in enumerate((0, 2, 4) * 3):
        src, dst = params[5 * (k // 3) + p], ws[k]
        if dst.shape != src.shape:
            zero(dst.at[:, src.shape[1]:])

    for load in loads[4:]:
        load.start()

    exchanges = [Exchange(grid, sems, counter) for _ in range(6)]
    barrier = pltpu.get_barrier_semaphore()
    for dr, dc in NEIGHBOURS:
        there = exchanges[0].exists(dr, dc)

        def greet(dr=dr, dc=dc):
            pl.semaphore_signal(barrier, inc=1, device_id={"row": row + dr, "col": col + dc}, device_id_type=MESH)

        pl.when(there)(greet)
    row_inner = jnp.logical_and(row > 0, row + 1 < cfg["rows"])
    col_inner = jnp.logical_and(col > 0, col + 1 < cfg["cols"])
    for row_peers, row_test in ((3, row_inner), (2, jnp.logical_not(row_inner))):
        for col_peers, col_test in ((3, col_inner), (2, jnp.logical_not(col_inner))):
            peers = row_peers * col_peers - 1
            pl.when(jnp.logical_and(row_test, col_test))(functools.partial(pl.semaphore_wait, barrier, peers))

    zin = [xs, zs[0], zs[1]]

    waited_loads = set()

    def wait_load(index):
        if index not in waited_loads:
            waited_loads.add(index)
            loads[index].wait()

    def flat(block):
        return block.reshape(-1, LANE)

    def stack(pieces):
        return pieces[0] if len(pieces) == 1 else jnp.concatenate(pieces, axis=0)

    def matrix(ref):
        value = ref[...]
        return value.reshape(-1, value.shape[-1])

    def times(lhs, ref, transposed):
        if transposed:
            return sum(lax.dot_general(lhs[:, t * ref.shape[2]:(t + 1) * ref.shape[2]], ref[t], (((1,), (1,)), ((), ())), preferred_element_type=jnp.float32)
                       for t in range(ref.shape[0]))
        return jnp.dot(lhs, matrix(ref), preferred_element_type=jnp.float32)

    def strided(src, ct, runs, kh, kw, c0, c1):
        up, lo = (1 if kh else 0), c0 + (1 if kw else 0)
        return stack([flat(src[ct, a + up:b + up, (kh + 1) % 2, lo:lo + c1 - c0, (kw + 1) % 2]) for a, b in runs])

    def centre(s, runs, c0, c1):
        src = zin[s]
        return jnp.concatenate([strided(src, ct, runs, 1, 1, c0, c1) for ct in range(src.shape[0])], axis=1)

    def down(s, rows, c0, c1):
        src, dst = zin[s], ys[s]
        wait_load(1 + 3 * s)
        taps = []
        for kh in range(3):
            for kw in range(3):
                for ct in range(src.shape[0]):
                    taps.append(strided(src, ct, rows, kh, kw, c0, c1))
        acc = times(jnp.concatenate(taps, axis=1), ws[3 * s], cfg["transposed"][3 * s])
        val = jnp.maximum(acc + params[5 * s + 1][...], 0.0).astype(dtype)
        n = images * (c1 - c0)
        for ct in range(dst.shape[0]):
            l1 = min(chans[s + 1] - ct * LANE, LANE)
            r = 0
            for a, b in rows:
                part = val[r * n:(r + b - a) * n, ct * LANE:ct * LANE + l1]
                dst[ct, a + 1:b + 1, c0 + 1:c1 + 1, :, 0:l1] = part.reshape(b - a, c1 - c0, images, l1)
                r += b - a

    def conv(s, rows, c0, c1):
        src = ys[s]
        wait_load(2 + 3 * s)
        wait_load(3 + 3 * s)
        taps = []
        for kh in range(3):
            for kw in range(3):
                for ct in range(src.shape[0]):
                    taps.append(stack([flat(src[ct, a + kh:b + kh, c0 + kw:c1 + kw]) for a, b in rows]))
        acc = times(jnp.concatenate(taps, axis=1), ws[3 * s + 1], cfg["transposed"][3 * s + 1])
        acc += times(centre(s, rows, c0, c1), ws[3 * s + 2], cfg["transposed"][3 * s + 2])
        val = jnp.maximum(acc + params[5 * s + 3][...], 0.0).astype(dtype)
        n = images * (c1 - c0)
        if s == 2:
            (a, b), = rows
            out_ref[a:b] = val.reshape(b - a, images, chans[3])
            return
        dst = zin[s + 1]
        for ct in range(dst.shape[0]):
            l1 = min(chans[s + 1] - ct * LANE, LANE)
            r = 0
            for a, b in rows:
                part = val[r * n:(r + b - a) * n, ct * LANE:ct * LANE + l1].reshape(b - a, c1 - c0, images, l1)
                r += b - a
                even, odd = a + a % 2, b - b % 2
                for c in range(c0, c1):
                    into = (c // 2 + 1, c % 2, slice(None), slice(0, l1))
                    if a < even:
                        dst[(ct, a // 2 + 1, 1) + into] = part[0, c - c0]
                    if odd > even:
                        dst[(ct, slice(even // 2 + 1, odd // 2 + 1), slice(None)) + into] = part[even - a:odd - a, c - c0].reshape((odd - even) // 2, 2, images, l1)
                    if odd < b and b - 1 >= even:
                        dst[(ct, odd // 2 + 1, 0) + into] = part[b - 1 - a, c - c0]

    def send_y_col(s, side, k, a, b):
        y, w = ys[s], width[s + 1]
        own, there = (w, 0) if side > 0 else (1, w + 1)
        exchanges[2 * s + 1].send(("c", side, k), 0, side, y.at[:, 1 + a:1 + b, own], y.at[:, 1 + a:1 + b, there])

    def send_y_row(s, side):
        y, h, w = ys[s], height[s + 1], width[s + 1]
        own, there = (h, 0) if side > 0 else (1, h + 1)
        ex = exchanges[2 * s + 1]
        ex.send(("r", side), side, 0, y.at[:, own, 1:w + 1], y.at[:, there, 1:w + 1])
        ex.send(("d", side, 1), side, 1, y.at[:, own, w], y.at[:, there, 0])
        ex.send(("d", side, -1), side, -1, y.at[:, own, 1], y.at[:, there, w + 1])

    def send_z_col(s, k, a, b):
        z, w = zin[s], width[s]
        exchanges[2 * s].send(("c", k), 0, 1, z.at[:, 1 + a // 2:1 + b // 2, :, w // 2, 1], z.at[:, 1 + a // 2:1 + b // 2, :, 0, 1])

    def send_z_row(s):
        z, h, w = zin[s], height[s], width[s]
        ex = exchanges[2 * s]
        ex.send("r", 1, 0, z.at[:, h // 2, 1, 1:], z.at[:, 0, 1, 1:])
        ex.send("d", 1, 1, z.at[:, h // 2, 1, w // 2, 1], z.at[:, 0, 1, 0, 1])

    def need_z_col(s, b):
        for k, (lo, hi) in enumerate(zcuts[s]):
            if lo < 2 * b:
                exchanges[2 * s].need(("c", k))

    def need_y_col(s, side, b):
        for k, (lo, hi) in enumerate(ycuts[s]):
            if lo < b + 1:
                exchanges[2 * s + 1].need(("c", side, k))

    def blocks(lo, hi, size):
        return [[(k, min(k + size, hi))] for k in range(lo, hi, size)]

    zcuts = [cut(height[s], cfg["zcut"][s], 2) for s in range(3)]
    ycuts = [cut(height[s + 1], cfg["ycut"][s]) for s in range(3)]

    h0, w0 = height[0], width[0]
    ex = exchanges[0]
    ex.send("r", 1, 0, x_hbm.at[h0 // 2 - 1, 1], xs.at[0, 0, 1, 1:])
    ex.send("d", 1, 1, x_hbm.at[h0 // 2 - 1, 1, w0 // 2 - 1, 1], xs.at[0, 0, 1, 0, 1])
    for k, (a, b) in enumerate(zcuts[0]):
        ex.send(("c", k), 0, 1, x_hbm.at[a // 2:b // 2, :, w0 // 2 - 1, 1], xs.at[0, 1 + a // 2:1 + b // 2, :, 0, 1])
    wait_load(0)

    h1, w1 = height[1], width[1]
    for rows in blocks(8, h1, 8):
        down(0, rows, 1, w1)
    ex.need("r")
    down(0, [(0, 8)], 1, w1)
    for k, (a, b) in enumerate(ycuts[0]):
        send_y_col(0, 1, k, a, b)
    for k, (a, b) in enumerate(ycuts[0]):
        need_z_col(0, b)
        if k == 0:
            ex.need("d")
        down(0, [(a, b)], 0, 1)
        send_y_col(0, -1, k, a, b)
        if k == 0:
            send_y_row(0, -1)
        if b == h1:
            send_y_row(0, 1)
        lo, hi = max(a - 1, 1), b - 1
        for rows in blocks(lo, hi, 8):
            conv(0, rows, 1, w1 - 1)
    ex = exchanges[1]
    ex.need(("r", -1), ("r", 1))
    conv(0, [(0, 1), (h1 - 1, h1)], 1, w1 - 1)
    for k, (a, b) in enumerate(zcuts[1]):
        need_y_col(0, -1, b)
        if k == 0:
            ex.need(("d", 1, -1))
        if b == h1:
            ex.need(("d", -1, -1))
        conv(0, [(a, b)], w1 - 1, w1)
        send_z_col(1, k, a, b)
    for k, (a, b) in enumerate(zcuts[1]):
        need_y_col(0, 1, b)
        if k == 0:
            ex.need(("d", 1, 1))
        if b == h1:
            ex.need(("d", -1, 1))
        conv(0, [(a, b)], 0, 1)
    send_z_row(1)

    for s in (1, 2):
        h, w = height[s + 1], width[s + 1]
        ex = exchanges[2 * s]
        ex.need("r")
        if w > 1:
            for rows in blocks(0, h, 12):
                down(s, rows, 1, w)
            for k, (a, b) in enumerate(ycuts[s]):
                send_y_col(s, 1, k, a, b)
        for k, (a, b) in enumerate(ycuts[s]):
            need_z_col(s, b)
            if k == 0:
                ex.need("d")
            down(s, [(a, b)], 0, 1)
            if w == 1:
                send_y_col(s, 1, k, a, b)
            send_y_col(s, -1, k, a, b)
        send_y_row(s, -1)
        send_y_row(s, 1)
        ex = exchanges[2 * s + 1]
        ex.need(("r", -1), ("r", 1))
        if s == 1:
            for k, (a, b) in enumerate(zcuts[2]):
                need_y_col(s, -1, b)
                if k == 0:
                    ex.need(("d", 1, -1))
                if b == h:
                    ex.need(("d", -1, -1))
                conv(s, [(a, b)], 1, w)
                send_z_col(2, k, a, b)
            for k, (a, b) in enumerate(zcuts[2]):
                need_y_col(s, 1, b)
                if k == 0:
                    ex.need(("d", 1, 1))
                if b == h:
                    ex.need(("d", -1, 1))
                conv(s, [(a, b)], 0, 1)
            send_z_row(2)
        else:
            need_y_col(s, 1, h)
            need_y_col(s, -1, h)
            ex.need(*[("d", i, j) for i in (-1, 1) for j in (-1, 1)])
            conv(s, [(0, h)], 0, 1)
    for ex in exchanges:
        ex.finish()


def solution(mesh):
    row_count = mesh.shape["row"]
    col_count = mesh.shape["col"]
    tile_spec = P("batch", "row", "col")

    def local_blocks(x_tile, *params):
        images, tile_h, tile_w, c0 = x_tile.shape
        chans = [c0] + [params[5 * s].shape[-1] for s in range(3)]
        height = [tile_h >> s for s in range(4)]
        width = [tile_w >> s for s in range(4)]
        x_in = jnp.transpose(x_tile, (1, 2, 0, 3)).reshape(tile_h // 2, 2, tile_w // 2, 2, images, c0)
        operands, transposed, wshapes = [], [], []
        for s in range(3):
            for p in range(5):
                value = params[5 * s + p]
                if p in (1, 3):
                    operands.append(value.reshape(1, -1))
                    continue
                k, n = value.shape[-2:]
                flip = k % LANE == 0 and n % LANE != 0
                value = value.reshape(-1, k, n)
                if flip:
                    value = jnp.swapaxes(value, 1, 2)
                    wshapes.append(value.shape)
                else:
                    wshapes.append((value.shape[0], tiles_of(k) * LANE, n))
                operands.append(value)
                transposed.append(flip)
        zcut, ycut = (4, 3, 2), (4, 2, 1)
        cfg = dict(chans=chans, height=height, width=width, rows=row_count, cols=col_count, images=images, transposed=transposed, zcut=zcut, ycut=ycut)
        messages = sum(zcut) + 2 * 3 + 2 * sum(ycut) + 3 * 6
        bf16 = jnp.bfloat16
        scratch = [pltpu.VMEM((1, tile_h // 2 + 1, 2, tile_w // 2 + 1, 2, images, LANE), bf16)]
        for s in (1, 2, 3):
            scratch.append(pltpu.VMEM((tiles_of(chans[s]), height[s] + 2, width[s] + 2, images, LANE), bf16))
        for s in (1, 2):
            scratch.append(pltpu.VMEM((tiles_of(chans[s]), height[s] // 2 + 1, 2, width[s] // 2 + 1, 2, images, LANE), bf16))
        for shape in wshapes:
            scratch.append(pltpu.VMEM(shape, bf16))
        scratch += [pltpu.SemaphoreType.DMA((10,)), pltpu.SemaphoreType.DMA((2, messages))]
        hbm = pl.BlockSpec(memory_space=pl.ANY)
        vmem = pl.BlockSpec(memory_space=pltpu.VMEM)
        out = pl.pallas_call(
            functools.partial(body, cfg),
            out_shape=jax.ShapeDtypeStruct((height[3], images, chans[3]), bf16),
            in_specs=[hbm] + [vmem if p in (1, 3) else hbm for _ in range(3) for p in range(5)],
            out_specs=vmem,
            scratch_shapes=scratch,
            compiler_params=pltpu.CompilerParams(collective_id=0, has_side_effects=True, vmem_limit_bytes=60 * 1024 * 1024),
            name="encoder",
        )(x_in, *operands)
        return jnp.transpose(out, (1, 0, 2))[:, :, None, :]

    return jax.shard_map(local_blocks, mesh=mesh, in_specs=(tile_spec,) + (P(),) * 15, out_specs=tile_spec, check_vma=False)
```

profile of v0, /device:TPU:101, one launch (start us, length us, event | category | flops | bytes accessed | tf_op | source)
XLA Modules:
  0.0 72.4 jit_solution(3568073346316844457)
XLA Ops:
  0.0 1.2 %reshape.55.refs_6_ = f32[1,320]{1,0:T(1,128)} reshape(f32[320]{0:T(512)} %param.23) | data formatting | bytes 2560 | tf_op jit(solution)/shard_map/reshape | solution.py:359
  1.2 1.2 %reshape.57.refs_8_ = f32[1,320]{1,0:T(1,128)} reshape(f32[320]{0:T(512)} %param.25) | data formatting | bytes 2560 | tf_op jit(solution)/shard_map/reshape | solution.py:359
  2.5 1.2 %reshape.60.refs_11_ = f32[1,320]{1,0:T(1,128)} reshape(f32[320]{0:T(512)} %param.28) | data formatting | bytes 2560 | tf_op jit(solution)/shard_map/reshape | solution.py:359
  3.7 1.3 %reshape.62.refs_13_ = f32[1,320]{1,0:T(1,128)} reshape(f32[320]{0:T(512)} %param.30) | data formatting | bytes 2560 | tf_op jit(solution)/shard_map/reshape | solution.py:359
  5.0 7.2 %copy.17 = bf16[96,8,16,128]{3,2,1,0:T(8,128)(2,1)} copy(bf16[96,8,16,128]{3,1,0,2:T(8,128)(2,1)} %bitcast.23) | data formatting | bytes 6291456 | tf_op jit(solution)/shard_map/transpose | solution.py:353
  12.2 58.6 %encoder.1 = bf16[12,16,320]{2,1,0:T(8,128)(2,1)} custom-call(bf16[48,2,4,2,16,128]{5,4,3,2,1,0:T(8,128)(2,1)} %bitcast.22, bf16[9,128,256]{2,1,0:T(8,128)(2,1)} %bitcast.29, f32[1,256]{1,0:T(1,128)} %bitcast.34, bf16[9,256,256]{2,1,0:T(8,128)(2,1)} %bitcast.28, f32[1,256]{1,0:T(1,128)} %bitcast.35, bf16[1,128,256]{2,1,0:T(8,128)(2,1)} %bitcast.33, ...), custom_call_target="tpu_custom_call" | custom-call | tf_op jit(solution)/shard_map/encoder/pallas_call | solution.py:385
  70.8 1.6 %copy.20 = bf16[16,12,1,320]{3,0,2,1:T(8,128)(2,1)} copy(bf16[16,12,1,320]{3,0,2,1:T(8,128)(2,1)} %bitcast.30) | data formatting | bytes 245760
where the time goes:
time: 72.6 us; the launch traced here: 72.4 us
  Pallas kernels  58.6 us (81%)
  local copies, waits for them, and re-layouts  13.8 us (19%)
    pallas_call x1, Pallas kernels, local_blocks(): pl.pallas_call(functools.partial(body, cfg), out_shape=jax.ShapeDtypeStru...  58.6 us
    transpose x1, local copies, waits for them, and re-layouts, local_blocks(): jnp.transpose(x_tile, (1, 2, 0, 3))  7.2 us
    reshape x4, local copies, waits for them, and re-layouts, local_blocks(): operands.append(value.reshape(1, -1))  4.97 us
    unnamed x1, local copies, waits for them, and re-layouts  1.59 us

commit v1 on v0

--- a/solution.py
+++ b/solution.py
@@ -65,7 +65,7 @@
 
 def body(cfg, x_hbm, *refs):
     params, refs = refs[:15], refs[15:]
-    out_ref, xs, ys, zs, ws, load_sems, sems = refs[0], refs[1], refs[2:5], refs[5:7], refs[7:16], refs[16], refs[17]
+    out_ref, raw, xs, ys, zs, ws, load_sems, sems = refs[0], refs[1], refs[2], refs[3:6], refs[6:8], refs[8:17], refs[17], refs[18]
     chans, height, width = cfg["chans"], cfg["height"], cfg["width"]
     row, col = lax.axis_index("row"), lax.axis_index("col")
     grid = (row, col, cfg["rows"], cfg["cols"])
@@ -73,14 +73,16 @@
     dtype = jnp.bfloat16
     images = cfg["images"]
 
-    loads = [pltpu.make_async_copy(x_hbm, xs.at[0, 1:, :, 1:], load_sems.at[0])]
+    xcuts = cut(height[0], cfg["zcut"][0], 2)
+    xloads = [pltpu.make_async_copy(x_hbm.at[:, a:b], raw.at[:, a:b], load_sems.at[9 + k]) for k, (a, b) in enumerate(xcuts)]
+    loads = []
     for stage in range(3):
         for k, p in enumerate((0, 2, 4)):
             src, dst = params[5 * stage + p], ws[3 * stage + k]
             if dst.shape != src.shape:
                 dst = dst.at[:, :src.shape[1]]
-            loads.append(pltpu.make_async_copy(src, dst, load_sems.at[1 + 3 * stage + k]))
-    for load in loads[:4]:
+            loads.append(pltpu.make_async_copy(src, dst, load_sems.at[3 * stage + k]))
+    for load in xloads + loads[:3]:
         load.start()
 
     def zero(ref):
@@ -101,7 +103,7 @@
         if dst.shape != src.shape:
             zero(dst.at[:, src.shape[1]:])
 
-    for load in loads[4:]:
+    for load in loads[3:]:
         load.start()
 
     exchanges = [Exchange(grid, sems, counter) for _ in range(6)]
@@ -155,14 +157,14 @@
 
     def down(s, rows, c0, c1):
         src, dst = zin[s], ys[s]
-        wait_load(1 + 3 * s)
+        wait_load(3 * s)
         taps = []
         for kh in range(3):
             for kw in range(3):
                 for ct in range(src.shape[0]):
                     taps.append(strided(src, ct, rows, kh, kw, c0, c1))
         acc = times(jnp.concatenate(taps, axis=1), ws[3 * s], cfg["transposed"][3 * s])
-        val = jnp.maximum(acc + params[5 * s + 1][...], 0.0).astype(dtype)
+        val = jnp.maximum(acc + params[5 * s + 1][...].reshape(1, -1), 0.0).astype(dtype)
         n = images * (c1 - c0)
         for ct in range(dst.shape[0]):
             l1 = min(chans[s + 1] - ct * LANE, LANE)
@@ -174,8 +176,8 @@
 
     def conv(s, rows, c0, c1):
         src = ys[s]
-        wait_load(2 + 3 * s)
-        wait_load(3 + 3 * s)
+        wait_load(3 * s + 1)
+        wait_load(3 * s + 2)
         taps = []
         for kh in range(3):
             for kw in range(3):
@@ -183,7 +185,7 @@
                     taps.append(stack([flat(src[ct, a + kh:b + kh, c0 + kw:c1 + kw]) for a, b in rows]))
         acc = times(jnp.concatenate(taps, axis=1), ws[3 * s + 1], cfg["transposed"][3 * s + 1])
         acc += times(centre(s, rows, c0, c1), ws[3 * s + 2], cfg["transposed"][3 * s + 2])
-        val = jnp.maximum(acc + params[5 * s + 3][...], 0.0).astype(dtype)
+        val = jnp.maximum(acc + params[5 * s + 3][...].reshape(1, -1), 0.0).astype(dtype)
         n = images * (c1 - c0)
         if s == 2:
             (a, b), = rows
@@ -245,13 +247,14 @@
     zcuts = [cut(height[s], cfg["zcut"][s], 2) for s in range(3)]
     ycuts = [cut(height[s + 1], cfg["ycut"][s]) for s in range(3)]
 
-    h0, w0 = height[0], width[0]
+    for k, (a, b) in enumerate(zcuts[0]):
+        xloads[k].wait()
+        for i in range(a, b):
+            tile = jnp.swapaxes(raw[:, i], 0, 1)
+            xs[0, i // 2 + 1, i % 2, 1:] = tile.reshape(width[0] // 2, 2, images, LANE)
+        send_z_col(0, k, a, b)
+    send_z_row(0)
     ex = exchanges[0]
-    ex.send("r", 1, 0, x_hbm.at[h0 // 2 - 1, 1], xs.at[0, 0, 1, 1:])
-    ex.send("d", 1, 1, x_hbm.at[h0 // 2 - 1, 1, w0 // 2 - 1, 1], xs.at[0, 0, 1, 0, 1])
-    for k, (a, b) in enumerate(zcuts[0]):
-        ex.send(("c", k), 0, 1, x_hbm.at[a // 2:b // 2, :, w0 // 2 - 1, 1], xs.at[0, 1 + a // 2:1 + b // 2, :, 0, 1])
-    wait_load(0)
 
     h1, w1 = height[1], width[1]
     for rows in blocks(8, h1, 8):
@@ -350,13 +353,12 @@
         chans = [c0] + [params[5 * s].shape[-1] for s in range(3)]
         height = [tile_h >> s for s in range(4)]
         width = [tile_w >> s for s in range(4)]
-        x_in = jnp.transpose(x_tile, (1, 2, 0, 3)).reshape(tile_h // 2, 2, tile_w // 2, 2, images, c0)
         operands, transposed, wshapes = [], [], []
         for s in range(3):
             for p in range(5):
                 value = params[5 * s + p]
                 if p in (1, 3):
-                    operands.append(value.reshape(1, -1))
+                    operands.append(value)
                     continue
                 k, n = value.shape[-2:]
                 flip = k % LANE == 0 and n % LANE != 0
@@ -372,14 +374,14 @@
         cfg = dict(chans=chans, height=height, width=width, rows=row_count, cols=col_count, images=images, transposed=transposed, zcut=zcut, ycut=ycut)
         messages = sum(zcut) + 2 * 3 + 2 * sum(ycut) + 3 * 6
         bf16 = jnp.bfloat16
-        scratch = [pltpu.VMEM((1, tile_h // 2 + 1, 2, tile_w // 2 + 1, 2, images, LANE), bf16)]
+        scratch = [pltpu.VMEM(x_tile.shape, bf16), pltpu.VMEM((1, tile_h // 2 + 1, 2, tile_w // 2 + 1, 2, images, LANE), bf16)]
         for s in (1, 2, 3):
             scratch.append(pltpu.VMEM((tiles_of(chans[s]), height[s] + 2, width[s] + 2, images, LANE), bf16))
         for s in (1, 2):
             scratch.append(pltpu.VMEM((tiles_of(chans[s]), height[s] // 2 + 1, 2, width[s] // 2 + 1, 2, images, LANE), bf16))
         for shape in wshapes:
             scratch.append(pltpu.VMEM(shape, bf16))
-        scratch += [pltpu.SemaphoreType.DMA((10,)), pltpu.SemaphoreType.DMA((2, messages))]
+        scratch += [pltpu.SemaphoreType.DMA((9 + zcut[0],)), pltpu.SemaphoreType.DMA((2, messages))]
         hbm = pl.BlockSpec(memory_space=pl.ANY)
         vmem = pl.BlockSpec(memory_space=pltpu.VMEM)
         out = pl.pallas_call(
@@ -390,7 +392,7 @@
             scratch_shapes=scratch,
             compiler_params=pltpu.CompilerParams(collective_id=0, has_side_effects=True, vmem_limit_bytes=60 * 1024 * 1024),
             name="encoder",
-        )(x_in, *operands)
+        )(x_tile, *operands)
         return jnp.transpose(out, (1, 0, 2))[:, :, None, :]
 
     return jax.shard_map(local_blocks, mesh=mesh, in_specs=(tile_spec,) + (P(),) * 15, out_specs=tile_spec, check_vma=False)

time: 72.6 us -> 61.6 us (0.85)
  local copies, waits for them, and re-layouts: 13.8 us -> 1.59 us
  Pallas kernels: 58.6 us -> 59.8 us
    transpose x1 -> x0, local copies, waits for them, and re-layouts: 7.2 us -> none  [local_blocks(): jnp.transpose(x_tile, (1, 2, 0, 3))]
    reshape x4 -> x0, local copies, waits for them, and re-layouts: 4.97 us -> none  [local_blocks(): operands.append(value.reshape(1, -1))]
    pallas_call x1, Pallas kernels: 58.6 us -> 59.8 us  [local_blocks(): pl.pallas_call(functools.partial(body, cfg), out_shape=jax.ShapeDtypeStru...]
where the time goes in v1:
time: 61.6 us; the launch traced here: 61.4 us
  Pallas kernels  59.8 us (97%)
  local copies, waits for them, and re-layouts  1.59 us (3%)
    pallas_call x1, Pallas kernels, local_blocks(): pl.pallas_call(functools.partial(body, cfg), out_shape=jax.ShapeDtypeStru...  59.8 us
    unnamed x1, local copies, waits for them, and re-layouts  1.59 us

profile of v1, /device:TPU:101, one launch (start us, length us, event | category | flops | bytes accessed | tf_op | source)
XLA Modules:
  0.0 61.4 jit_solution(4146005261894595597)
XLA Ops:
  0.0 59.8 %encoder.1 = bf16[12,16,320]{2,1,0:T(8,128)(2,1)} custom-call(bf16[16,96,8,128]{3,2,1,0:T(8,128)(2,1)} %x_hbm.1, bf16[9,128,256]{2,1,0:T(8,128)(2,1)} %bitcast.23, f32[256]{0:T(256)} %refs_1_.1, bf16[9,256,256]{2,1,0:T(8,128)(2,1)} %bitcast.22, f32[256]{0:T(256)} %refs_3_.1, bf16[1,128,256]{2,1,0:T(8,128)(2,1)} %bitcast.27, bf16[9,320,256]{2,1,0:T(8,128)(2,1)} %bitcast.21, ...), custom_call_target="tpu_custom_call" | custom-call | tf_op jit(solution)/shard_map/encoder/pallas_call | solution.py:387
  59.9 1.6 %copy.19 = bf16[16,12,1,320]{3,0,2,1:T(8,128)(2,1)} copy(bf16[16,12,1,320]{3,0,2,1:T(8,128)(2,1)} %bitcast.24) | data formatting | bytes 245760

commit v2 on v1

--- a/solution.py
+++ b/solution.py
@@ -65,7 +65,9 @@
 
 def body(cfg, x_hbm, *refs):
     params, refs = refs[:15], refs[15:]
-    out_ref, raw, xs, ys, zs, ws, load_sems, sems = refs[0], refs[1], refs[2], refs[3:6], refs[6:8], refs[8:17], refs[17], refs[18]
+    out_ref, raw, xs, ys, zs, ws, load_sems, sems = refs[0], refs[1], refs[2], refs[3:6], refs[6:8], refs[8:17], refs[20], refs[21]
+    packs = refs[17:20]
+    packs = (packs[1], packs[0], None, packs[2])
     chans, height, width = cfg["chans"], cfg["height"], cfg["width"]
     row, col = lax.axis_index("row"), lax.axis_index("col")
     grid = (row, col, cfg["rows"], cfg["cols"])
@@ -115,13 +117,6 @@
             pl.semaphore_signal(barrier, inc=1, device_id={"row": row + dr, "col": col + dc}, device_id_type=MESH)
 
         pl.when(there)(greet)
-    row_inner = jnp.logical_and(row > 0, row + 1 < cfg["rows"])
-    col_inner = jnp.logical_and(col > 0, col + 1 < cfg["cols"])
-    for row_peers, row_test in ((3, row_inner), (2, jnp.logical_not(row_inner))):
-        for col_peers, col_test in ((3, col_inner), (2, jnp.logical_not(col_inner))):
-            peers = row_peers * col_peers - 1
-            pl.when(jnp.logical_and(row_test, col_test))(functools.partial(pl.semaphore_wait, barrier, peers))
-
     zin = [xs, zs[0], zs[1]]
 
     waited_loads = set()
@@ -208,10 +203,50 @@
                     if odd < b and b - 1 >= even:
                         dst[(ct, odd // 2 + 1, 0) + into] = part[b - 1 - a, c - c0]
 
+    def halves(tile):
+        return pltpu.roll(tile.astype(jnp.float32), LANE // 2, tile.ndim - 1).astype(dtype)
+
+    lower = lax.broadcasted_iota(jnp.int32, (1, images, LANE), 2) < LANE // 2
+
+    def send_column(ex, key, side, buf, packed, own, there, count, k):
+        full = buf.shape[0] if packed is None else buf.shape[0] - 1
+        ex.send(key, 0, side, own(slice(0, full)), there(slice(0, full)))
+        if packed is not None:
+            out, into = packed
+            rest = own(full)[...].reshape(count // 2, 2, images, LANE)
+            out[...] = jnp.where(lower, rest[:, 0], halves(rest[:, 1]))
+            ex.send(key + ("rest",), 0, side, out, into)
+
+    def unpack(into, packed, count):
+        tile = packed[1][...]
+        none = jnp.zeros_like(tile)
+        rest = jnp.stack([jnp.where(lower, tile, none), jnp.where(lower, halves(tile), none)], axis=1)
+        into[...] = rest.reshape(into.shape)
+
+    def need_column(ex, key, side, into, packed, count):
+        if key in ex.waited:
+            return
+        ex.need(key)
+        if packed is not None:
+            ex.need(key + ("rest",))
+            pl.when(ex.exists(0, -side))(functools.partial(unpack, into, packed, count))
+
+    def y_packed(s, side, a, b):
+        if s == 0:
+            return None
+        at = 0 if side > 0 else 1
+        return packs[2 * s - 1].at[0, at, a // 2:b // 2], packs[2 * s - 1].at[1, at, a // 2:b // 2]
+
+    def z_packed(s, a, b):
+        if s < 2:
+            return None
+        return packs[0].at[0, a // 2:b // 2], packs[0].at[1, a // 2:b // 2]
+
     def send_y_col(s, side, k, a, b):
         y, w = ys[s], width[s + 1]
         own, there = (w, 0) if side > 0 else (1, w + 1)
-        exchanges[2 * s + 1].send(("c", side, k), 0, side, y.at[:, 1 + a:1 + b, own], y.at[:, 1 + a:1 + b, there])
+        send_column(exchanges[2 * s + 1], ("c", side, k), side, y, y_packed(s, side, a, b),
+                    lambda ct: y.at[ct, 1 + a:1 + b, own], lambda ct: y.at[ct, 1 + a:1 + b, there], b - a, k)
 
     def send_y_row(s, side):
         y, h, w = ys[s], height[s + 1], width[s + 1]
@@ -223,7 +258,9 @@
 
     def send_z_col(s, k, a, b):
         z, w = zin[s], width[s]
-        exchanges[2 * s].send(("c", k), 0, 1, z.at[:, 1 + a // 2:1 + b // 2, :, w // 2, 1], z.at[:, 1 + a // 2:1 + b // 2, :, 0, 1])
+        rows = slice(1 + a // 2, 1 + b // 2)
+        send_column(exchanges[2 * s], ("c", k), 1, z, z_packed(s, a, b),
+                    lambda ct: z.at[ct, rows, :, w // 2, 1], lambda ct: z.at[ct, rows, :, 0, 1], b - a, k)
 
     def send_z_row(s):
         z, h, w = zin[s], height[s], width[s]
@@ -234,24 +271,35 @@
     def need_z_col(s, b):
         for k, (lo, hi) in enumerate(zcuts[s]):
             if lo < 2 * b:
-                exchanges[2 * s].need(("c", k))
+                z = zin[s]
+                need_column(exchanges[2 * s], ("c", k), 1, z.at[z.shape[0] - 1, 1 + lo // 2:1 + hi // 2, :, 0, 1], z_packed(s, lo, hi), hi - lo)
 
     def need_y_col(s, side, b):
         for k, (lo, hi) in enumerate(ycuts[s]):
             if lo < b + 1:
-                exchanges[2 * s + 1].need(("c", side, k))
+                y = ys[s]
+                need_column(exchanges[2 * s + 1], ("c", side, k), side, y.at[y.shape[0] - 1, 1 + lo:1 + hi, 0 if side > 0 else width[s + 1] + 1], y_packed(s, side, lo, hi), hi - lo)
 
     def blocks(lo, hi, size):
         return [[(k, min(k + size, hi))] for k in range(lo, hi, size)]
 
     zcuts = [cut(height[s], cfg["zcut"][s], 2) for s in range(3)]
-    ycuts = [cut(height[s + 1], cfg["ycut"][s]) for s in range(3)]
+    ycuts = [cut(height[s + 1], cfg["ycut"][s], 2) for s in range(3)]
 
     for k, (a, b) in enumerate(zcuts[0]):
         xloads[k].wait()
         for i in range(a, b):
             tile = jnp.swapaxes(raw[:, i], 0, 1)
             xs[0, i // 2 + 1, i % 2, 1:] = tile.reshape(width[0] // 2, 2, images, LANE)
+
+    row_inner = jnp.logical_and(row > 0, row + 1 < cfg["rows"])
+    col_inner = jnp.logical_and(col > 0, col + 1 < cfg["cols"])
+    for row_peers, row_test in ((3, row_inner), (2, jnp.logical_not(row_inner))):
+        for col_peers, col_test in ((3, col_inner), (2, jnp.logical_not(col_inner))):
+            peers = row_peers * col_peers - 1
+            pl.when(jnp.logical_and(row_test, col_test))(functools.partial(pl.semaphore_wait, barrier, peers))
+
+    for k, (a, b) in enumerate(zcuts[0]):
         send_z_col(0, k, a, b)
     send_z_row(0)
     ex = exchanges[0]
@@ -303,16 +351,13 @@
         if w > 1:
             for rows in blocks(0, h, 12):
                 down(s, rows, 1, w)
-            for k, (a, b) in enumerate(ycuts[s]):
-                send_y_col(s, 1, k, a, b)
         for k, (a, b) in enumerate(ycuts[s]):
             need_z_col(s, b)
             if k == 0:
                 ex.need("d")
             down(s, [(a, b)], 0, 1)
-            if w == 1:
-                send_y_col(s, 1, k, a, b)
             send_y_col(s, -1, k, a, b)
+            send_y_col(s, 1, k, a, b)
         send_y_row(s, -1)
         send_y_row(s, 1)
         ex = exchanges[2 * s + 1]
@@ -372,7 +417,7 @@
                 transposed.append(flip)
         zcut, ycut = (4, 3, 2), (4, 2, 1)
         cfg = dict(chans=chans, height=height, width=width, rows=row_count, cols=col_count, images=images, transposed=transposed, zcut=zcut, ycut=ycut)
-        messages = sum(zcut) + 2 * 3 + 2 * sum(ycut) + 3 * 6
+        messages = 2 * sum(zcut) + 2 * 3 + 4 * sum(ycut) + 3 * 6
         bf16 = jnp.bfloat16
         scratch = [pltpu.VMEM(x_tile.shape, bf16), pltpu.VMEM((1, tile_h // 2 + 1, 2, tile_w // 2 + 1, 2, images, LANE), bf16)]
         for s in (1, 2, 3):
@@ -381,6 +426,9 @@
             scratch.append(pltpu.VMEM((tiles_of(chans[s]), height[s] // 2 + 1, 2, width[s] // 2 + 1, 2, images, LANE), bf16))
         for shape in wshapes:
             scratch.append(pltpu.VMEM(shape, bf16))
+        scratch.append(pltpu.VMEM((2, 2, height[2] // 2, images, LANE), bf16))
+        scratch.append(pltpu.VMEM((2, height[2] // 2, images, LANE), bf16))
+        scratch.append(pltpu.VMEM((2, 2, height[3] // 2, images, LANE), bf16))
         scratch += [pltpu.SemaphoreType.DMA((9 + zcut[0],)), pltpu.SemaphoreType.DMA((2, messages))]
         hbm = pl.BlockSpec(memory_space=pl.ANY)
         vmem = pl.BlockSpec(memory_space=pltpu.VMEM)

time: 61.6 us -> 59.2 us (0.961)
  Pallas kernels: 59.8 us -> 57.5 us
    pallas_call x1, Pallas kernels: 59.8 us -> 57.5 us  [local_blocks(): pl.pallas_call(functools.partial(body, cfg), out_shape=jax.ShapeDtypeStru...]
where the time goes in v2:
time: 59.2 us; the launch traced here: 59.1 us
  Pallas kernels  57.5 us (97%)
  local copies, waits for them, and re-layouts  1.59 us (3%)
    pallas_call x1, Pallas kernels, local_blocks(): pl.pallas_call(functools.partial(body, cfg), out_shape=jax.ShapeDtypeStru...  57.5 us
    unnamed x1, local copies, waits for them, and re-layouts  1.59 us

profile of v2, /device:TPU:101, one launch (start us, length us, event | category | flops | bytes accessed | tf_op | source)
XLA Modules:
  0.0 59.1 jit_solution(14082609122772914188)
XLA Ops:
  0.0 57.5 %encoder.1 = bf16[12,16,320]{2,1,0:T(8,128)(2,1)} custom-call(bf16[16,96,8,128]{3,2,1,0:T(8,128)(2,1)} %x_hbm.1, bf16[9,128,256]{2,1,0:T(8,128)(2,1)} %bitcast.23, f32[256]{0:T(256)} %refs_1_.1, bf16[9,256,256]{2,1,0:T(8,128)(2,1)} %bitcast.22, f32[256]{0:T(256)} %refs_3_.1, bf16[1,128,256]{2,1,0:T(8,128)(2,1)} %bitcast.27, bf16[9,320,256]{2,1,0:T(8,128)(2,1)} %bitcast.21, ...), custom_call_target="tpu_custom_call" | custom-call | tf_op jit(solution)/shard_map/encoder/pallas_call | solution.py:435
  57.5 1.6 %copy.19 = bf16[16,12,1,320]{3,0,2,1:T(8,128)(2,1)} copy(bf16[16,12,1,320]{3,0,2,1:T(8,128)(2,1)} %bitcast.24) | data formatting | bytes 245760

commit v3 on v1

v3 whole, which is shorter than its diff:
```python
import functools

import jax
import jax.numpy as jnp
from jax import lax
from jax.experimental import pallas as pl
from jax.experimental.pallas import tpu as pltpu
from jax.sharding import PartitionSpec as P

LANE = 128
MESH = pl.DeviceIdType.MESH
NEIGHBOURS = [(dr, dc) for dr in range(-1, 2) for dc in range(-1, 2) if dr or dc]


def tiles_of(channels):
    return -(-channels // LANE)


def cut(count, pieces, unit=1):
    bounds = [round(count * k / pieces / unit) * unit for k in range(pieces + 1)]
    return [(a, b) for a, b in zip(bounds, bounds[1:]) if b > a]


WEIGHTS = (0, 2, 4)
PACKS = [("y", s, name) for s in range(1, 3) for name in ("left", "right")] + [("z", 2, "left")]


class Exchange:
    def __init__(self, grid, sems, counter, known):
        self.grid, self.sems, self.counter = grid, sems, counter
        self.copies = {}
        self.known = known
        self.landing = {}
        self.waited = set()

    def exists(self, dr, dc):
        if (dr, dc) not in self.known:
            row, col, row_count, col_count = self.grid
            tests = []
            if dr:
                tests.append(row + 1 < row_count if dr > 0 else row > 0)
            if dc:
                tests.append(col + 1 < col_count if dc > 0 else col > 0)
            self.known[dr, dc] = functools.reduce(jnp.logical_and, tests)
        return self.known[dr, dc]

    def arrives(self, key):
        dr, dc = self.copies[key][1:]
        return self.exists(-dr, -dc)

    def send(self, key, dr, dc, src, dst, before=None, then=None):
        row, col = self.grid[:2]
        copies = []
        for name, source, target in ((key, src, dst),) + (then or ()):
            index = self.counter[0]
            self.counter[0] += 1
            copy = pltpu.make_async_remote_copy(
                src_ref=source, dst_ref=target, send_sem=self.sems.at[0, index], recv_sem=self.sems.at[1, index],
                device_id={"row": row + dr, "col": col + dc}, device_id_type=MESH)
            self.copies[name] = (copy, dr, dc)
            copies.append(copy)

        def start():
            copies[0].start()
            if before is not None:
                before()
            for copy in copies[1:]:
                copy.start()

        pl.when(self.exists(dr, dc))(start)

    def together(self, groups):
        for test, waits in groups:
            def wait(waits=waits):
                for one in waits:
                    one()

            pl.when(test)(wait)

    def need(self, *keys, after=None):
        groups = {}
        for key in keys:
            if key not in self.waited:
                self.waited.add(key)
                test = self.arrives(key)
                groups.setdefault(id(test), (test, []))[1].append(self.copies[key][0].wait_recv)
        if after is not None:
            for test, waits in groups.values():
                waits.append(after)
        self.together(groups.values())

    def sends(self):
        assert self.waited == set(self.copies)
        return [(self.exists(dr, dc), copy.wait_send) for copy, dr, dc in self.copies.values()]


def body(cfg, x_hbm, *refs):
    params, refs = refs[:15], refs[15:]
    out_ref, raw, xs, y1, y2, y3, z1, z2, *ws, packs, load_sems, sems = refs
    ys, zs = (y1, y2, y3), (z1, z2)
    chans, height, width = cfg["chans"], cfg["height"], cfg["width"]
    row, col = lax.axis_index("row"), lax.axis_index("col")
    grid = (row, col, cfg["rows"], cfg["cols"])
    counter = [0]
    known = {}
    dtype = jnp.bfloat16
    images = cfg["images"]

    xcuts = cut(height[0], cfg["zcut"][0], 2)
    xloads = [pltpu.make_async_copy(x_hbm.at[:, a:b], raw.at[:, a:b], load_sems.at[9 + k]) for k, (a, b) in enumerate(xcuts)]
    loads = []
    for stage in range(3):
        for k, p in enumerate(WEIGHTS):
            src, dst = params[5 * stage + p], ws[3 * stage + k]
            if dst.shape != src.shape:
                dst = dst.at[:, :src.shape[1]]
            loads.append(pltpu.make_async_copy(src, dst, load_sems.at[3 * stage + k]))
    for load in xloads + loads[:3]:
        load.start()

    def zero(ref):
        ref[...] = jnp.zeros(ref.shape, ref.dtype)

    for buf in (xs,) + tuple(zs):
        zero(buf.at[:, 0, 1])
        zero(buf.at[:, :, :, 0, 1])
    for s, buf in enumerate(ys):
        zero(buf.at[:, 0:1])
        zero(buf.at[:, -1:])
        zero(buf.at[:, :, 0:1])
        zero(buf.at[:, :, width[s + 1] + 1:])
    for buf in tuple(ys[1:]) + tuple(zs[1:]):
        zero(buf.at[buf.shape[0] - 1:])
    for k, p in enumerate(WEIGHTS * 3):
        src, dst = params[5 * (k // 3) + p], ws[k]
        if dst.shape != src.shape:
            zero(dst.at[:, src.shape[1]:])

    for load in loads[3:]:
        load.start()

    exchanges = [Exchange(grid, sems, counter, known) for _ in range(6)]
    barrier = pltpu.get_barrier_semaphore()
    for dr, dc in NEIGHBOURS:
        there = exchanges[0].exists(dr, dc)

        def greet(dr=dr, dc=dc):
            pl.semaphore_signal(barrier, inc=1, device_id={"row": row + dr, "col": col + dc}, device_id_type=MESH)

        pl.when(there)(greet)
    zin = [xs, zs[0], zs[1]]

    waited_loads = set()

    def wait_load(index):
        if index not in waited_loads:
            waited_loads.add(index)
            loads[index].wait()

    def flat(block):
        return block.reshape(-1, LANE)

    def stack(pieces):
        return pieces[0] if len(pieces) == 1 else jnp.concatenate(pieces, axis=0)

    def matrix(ref):
        value = ref[...]
        return value.reshape(-1, value.shape[-1])

    def times(lhs, ref, transposed):
        if transposed:
            return sum(lax.dot_general(lhs[:, t * ref.shape[2]:(t + 1) * ref.shape[2]], ref[t], (((1,), (1,)), ((), ())), preferred_element_type=jnp.float32)
                       for t in range(ref.shape[0]))
        return jnp.dot(lhs, matrix(ref), preferred_element_type=jnp.float32)

    def strided(src, ct, runs, kh, kw, c0, nc):
        up, lo = (1 if kh else 0), c0 + (1 if kw else 0)
        return stack([flat(src[ct, a + up:b + up, (kh + 1) % 2, pl.ds(lo, nc), (kw + 1) % 2]) for a, b in runs])

    def centre(s, runs, c0, nc):
        src = zin[s]
        return jnp.concatenate([strided(src, ct, runs, 1, 1, c0, nc) for ct in range(src.shape[0])], axis=1)

    def down(s, rows, c0, nc=1):
        src, dst = zin[s], ys[s]
        wait_load(3 * s)
        taps = []
        for kh in range(3):
            for kw in range(3):
                for ct in range(src.shape[0]):
                    taps.append(strided(src, ct, rows, kh, kw, c0, nc))
        acc = times(jnp.concatenate(taps, axis=1), ws[3 * s], cfg["transposed"][3 * s])
        val = jnp.maximum(acc + params[5 * s + 1][...].reshape(1, -1), 0.0).astype(dtype)
        n = images * nc
        for ct in range(dst.shape[0]):
            l1 = min(chans[s + 1] - ct * LANE, LANE)
            r = 0
            for a, b in rows:
                part = val[r * n:(r + b - a) * n, ct * LANE:ct * LANE + l1]
                dst[ct, a + 1:b + 1, pl.ds(c0 + 1, nc), :, 0:l1] = part.reshape(b - a, nc, images, l1)
                r += b - a

    def conv(s, rows, c0, nc=1):
        src = ys[s]
        wait_load(3 * s + 1)
        wait_load(3 * s + 2)
        taps = []
        for kh in range(3):
            for kw in range(3):
                for ct in range(src.shape[0]):
                    taps.append(stack([flat(src[ct, a + kh:b + kh, pl.ds(c0 + kw, nc)]) for a, b in rows]))
        acc = times(jnp.concatenate(taps, axis=1), ws[3 * s + 1], cfg["transposed"][3 * s + 1])
        acc += times(centre(s, rows, c0, nc), ws[3 * s + 2], cfg["transposed"][3 * s + 2])
        val = jnp.maximum(acc + params[5 * s + 3][...].reshape(1, -1), 0.0).astype(dtype)
        n = images * nc
        if s == 2:
            (a, b), = rows
            out_ref[a:b] = val.reshape(b - a, images, chans[3])
            return
        dst = zin[s + 1]
        for ct in range(dst.shape[0]):
            l1 = min(chans[s + 1] - ct * LANE, LANE)
            r = 0
            for a, b in rows:
                part = val[r * n:(r + b - a) * n, ct * LANE:ct * LANE + l1].reshape(b - a, nc, images, l1)
                r += b - a
                even, odd = a + a % 2, b - b % 2
                for j in range(nc):
                    into = (lax.div(c0 + j, 2) + 1, lax.rem(c0 + j, 2), slice(None), slice(0, l1))
                    if a < even:
                        dst[(ct, a // 2 + 1, 1) + into] = part[0, j]
                    if odd > even:
                        dst[(ct, slice(even // 2 + 1, odd // 2 + 1), slice(None)) + into] = part[even - a:odd - a, j].reshape((odd - even) // 2, 2, images, l1)
                    if odd < b and b - 1 >= even:
                        dst[(ct, odd // 2 + 1, 0) + into] = part[b - 1 - a, j]

    def halves(tile):
        return pltpu.roll(tile.astype(jnp.float32), LANE // 2, tile.ndim - 1).astype(dtype)

    lower = lax.broadcasted_iota(jnp.int32, (1, images, LANE), 2) < LANE // 2

    def send_column(ex, key, side, packed, own, there, last, count):
        full = last + 1 if packed is None else last
        if packed is None:
            ex.send(key, 0, side, own(slice(0, full)), there(slice(0, full)))
        else:
            out, into = packed

            def pack():
                rest = own(full)[...].reshape(count // 2, 2, images, LANE)
                out[...] = jnp.where(lower, rest[:, 0], halves(rest[:, 1]))

            ex.send(key, 0, side, own(slice(0, full)), there(slice(0, full)), pack, ((key + ("rest",), out, into),))
        ex.landing[key] = (there(last), packed)

    def need_column(ex, key):
        if key in ex.waited:
            return
        into, packed = ex.landing[key]
        if packed is None:
            ex.need(key)
            return

        def unpack():
            tile = packed[1][...]
            none = jnp.zeros_like(tile)
            rest = jnp.stack([jnp.where(lower, tile, none), jnp.where(lower, halves(tile), none)], axis=1)
            into[...] = rest.reshape(into.shape)

        ex.need(key, key + ("rest",), after=unpack)

    def packs_of(key, a, b):
        if key not in PACKS:
            return None
        return tuple(packs.at[way, PACKS.index(key), a // 2:b // 2] for way in range(2))

    def send_y_col(s, name, side, k, own, there):
        a, b = ycuts[s][k]
        y = ys[s]
        packed = packs_of(("y", s, name), a, b)
        send_column(exchanges[2 * s + 1], (name, k), side, packed, lambda ct: y.at[ct, 1 + a:1 + b, 1 + own],
                    lambda ct: y.at[ct, 1 + a:1 + b, 1 + there], y.shape[0] - 1, b - a)

    def send_z_col(s, name, side, k, own, there):
        a, b = zcuts[s][k]
        z = zin[s]
        rows = slice(1 + a // 2, 1 + b // 2)
        packed = packs_of(("z", s, name), a, b)
        send_column(exchanges[2 * s], (name, k), side, packed, lambda ct: z.at[ct, rows, :, (own + 2) // 2, own % 2],
                    lambda ct: z.at[ct, rows, :, (there + 2) // 2, there % 2], z.shape[0] - 1, b - a)

    def send_y_rows(s, side):
        y, h, w = ys[s], height[s + 1], width[s + 1]
        own, there = (h, 0) if side > 0 else (1, h + 1)
        ex = exchanges[2 * s + 1]
        ex.send(("row", "r", side), side, 0, y.at[:, own, 1:w + 1], y.at[:, there, 1:w + 1])
        ex.send(("corner", "left", side), side, 1, y.at[:, own, w], y.at[:, there, 0])
        ex.send(("corner", "right", side), side, -1, y.at[:, own, 1], y.at[:, there, w + 1])

    def send_z_rows(s):
        z, h, w = zin[s], height[s] // 2, width[s] // 2
        ex = exchanges[2 * s]
        ex.send("row", 1, 0, z.at[:, h, 1, 1:], z.at[:, 0, 1, 1:])
        ex.send("corner", 1, 1, z.at[:, h, 1, w, 1], z.at[:, 0, 1, 0, 1])

    def need_corners(s, name):
        exchanges[2 * s + 1].need(("corner", name, -1), ("corner", name, 1))

    def need_z(s, name, b):
        for k, (lo, hi) in enumerate(zcuts[s]):
            if lo < 2 * b:
                need_column(exchanges[2 * s], (name, k))

    def need_y(s, name, b):
        for k, (lo, hi) in enumerate(ycuts[s]):
            if lo < b + 1:
                need_column(exchanges[2 * s + 1], (name, k))

    def blocks(lo, hi, size):
        return [[(k, min(k + size, hi))] for k in range(lo, hi, size)]

    zcuts = [cut(height[s], cfg["zcut"][s], 2) for s in range(3)]
    ycuts = [cut(height[s + 1], cfg["ycut"][s], 2) for s in range(3)]

    def turn(k):
        xloads[k].wait()
        for i in range(*zcuts[0][k]):
            tile = jnp.swapaxes(raw[:, i], 0, 1)
            xs[0, i // 2 + 1, i % 2, 1:1 + width[0] // 2] = tile.reshape(width[0] // 2, 2, images, LANE)

    turn(0)
    row_inner = jnp.logical_and(row > 0, row + 1 < cfg["rows"])
    col_inner = jnp.logical_and(col > 0, col + 1 < cfg["cols"])
    for rows, row_test in ((3, row_inner), (2, jnp.logical_not(row_inner))):
        for cols, col_test in ((3, col_inner), (2, jnp.logical_not(col_inner))):
            pl.when(jnp.logical_and(row_test, col_test))(functools.partial(pl.semaphore_wait, barrier, rows * cols - 1))

    w0, w1, w2 = width[:3]
    h1, h2, h3 = height[1:]
    for k in range(len(zcuts[0])):
        if k:
            turn(k)
        send_z_col(0, "left", 1, k, w0 - 1, -1)
    send_z_rows(0)

    ex = exchanges[0]
    for rows in blocks(8, h1, 8):
        down(0, rows, 1, w1 - 1)
    ex.need("row")
    down(0, [(0, 8)], 1, w1 - 1)
    for k in range(len(ycuts[0])):
        send_y_col(0, "left", 1, k, w1 - 1, -1)
    for k, (a, b) in enumerate(ycuts[0]):
        need_z(0, "left", b)
        ex.need("corner")
        down(0, [(a, b)], 0)
        send_y_col(0, "right", -1, k, 0, w1)
        if k == 0:
            send_y_rows(0, -1)
        if b == h1:
            send_y_rows(0, 1)
        for rows in blocks(max(a - 1, 1), b - 1, 8):
            conv(0, rows, 1, w1 - 2)
    exchanges[1].need(("row", "r", -1), ("row", "r", 1))
    conv(0, [(0, 1), (h1 - 1, h1)], 1, w1 - 2)
    need_corners(0, "right")
    for k, (a, b) in enumerate(zcuts[1]):
        need_y(0, "right", b)
        conv(0, [(a, b)], w1 - 1)
        send_z_col(1, "left", 1, k, w1 - 1, -1)
    need_corners(0, "left")
    for k, (a, b) in enumerate(zcuts[1]):
        need_y(0, "left", b)
        conv(0, [(a, b)], 0)
    send_z_rows(1)

    ex = exchanges[2]
    ex.need("row")
    for rows in blocks(0, h2, 12):
        down(1, rows, 1, w2 - 1)
    for k, (a, b) in enumerate(ycuts[1]):
        need_z(1, "left", b)
        ex.need("corner")
        down(1, [(a, b)], 0)
        send_y_col(1, "right", -1, k, 0, w2)
        send_y_col(1, "left", 1, k, w2 - 1, -1)
        if k == 0:
            send_y_rows(1, -1)
        if b == h2:
            send_y_rows(1, 1)
    exchanges[3].need(("row", "r", -1), ("row", "r", 1))
    need_corners(1, "right")
    for k, (a, b) in enumerate(zcuts[2]):
        need_y(1, "right", b)
        conv(1, [(a, b)], 1, w2 - 1)
        send_z_col(2, "left", 1, k, w2 - 1, -1)
    need_corners(1, "left")
    for k, (a, b) in enumerate(zcuts[2]):
        need_y(1, "left", b)
        conv(1, [(a, b)], 0)
    send_z_rows(2)

    ex = exchanges[4]
    ex.need("row")
    for k, (a, b) in enumerate(ycuts[2]):
        need_z(2, "left", b)
        ex.need("corner")
        down(2, [(a, b)], 0)
        send_y_col(2, "right", -1, k, 0, 1)
        send_y_col(2, "left", 1, k, 0, -1)
        if k == 0:
            send_y_rows(2, -1)
        if b == h3:
            send_y_rows(2, 1)
    exchanges[5].need(("row", "r", -1), ("row", "r", 1))
    need_corners(2, "left")
    need_corners(2, "right")
    need_y(2, "left", h3)
    need_y(2, "right", h3)
    conv(2, [(0, h3)], 0)
    assert counter[0] == sems.shape[1]
    groups = {}
    for ex in exchanges:
        for test, wait in ex.sends():
            groups.setdefault(id(test), (test, []))[1].append(wait)
    ex.together(groups.values())


def solution(mesh):
    row_count = mesh.shape["row"]
    col_count = mesh.shape["col"]
    tile_spec = P("batch", "row", "col")

    def local_blocks(x_tile, *params):
        images, tile_h, tile_w, c0 = x_tile.shape
        chans = [c0] + [params[5 * s].shape[-1] for s in range(3)]
        height = [tile_h >> s for s in range(4)]
        width = [tile_w >> s for s in range(4)]
        operands, transposed, wshapes = [], [], []
        for s in range(3):
            for p in range(5):
                value = params[5 * s + p]
                if p in (1, 3):
                    operands.append(value)
                    continue
                k, n = value.shape[-2:]
                flip = k % LANE == 0 and n % LANE != 0
                value = value.reshape(-1, k, n)
                if flip:
                    value = jnp.swapaxes(value, 1, 2)
                    wshapes.append(value.shape)
                else:
                    wshapes.append((value.shape[0], tiles_of(k) * LANE, n))
                operands.append(value)
                transposed.append(flip)
        zcut, ycut = (4, 3, 3), (4, 3, 2)
        cfg = dict(chans=chans, height=height, width=width, rows=row_count, cols=col_count, images=images, transposed=transposed, zcut=zcut, ycut=ycut)
        messages = 65
        bf16 = jnp.bfloat16
        scratch = [pltpu.VMEM(x_tile.shape, bf16), pltpu.VMEM((1, tile_h // 2 + 1, 2, tile_w // 2 + 1, 2, images, LANE), bf16)]
        for s in (1, 2, 3):
            scratch.append(pltpu.VMEM((tiles_of(chans[s]), height[s] + 2, width[s] + 2, images, LANE), bf16))
        for s in (1, 2):
            scratch.append(pltpu.VMEM((tiles_of(chans[s]), height[s] // 2 + 1, 2, width[s] // 2 + 1, 2, images, LANE), bf16))
        for shape in wshapes:
            scratch.append(pltpu.VMEM(shape, bf16))
        scratch.append(pltpu.VMEM((2, len(PACKS), height[2] // 2, images, LANE), bf16))
        scratch += [pltpu.SemaphoreType.DMA((9 + zcut[0],)), pltpu.SemaphoreType.DMA((2, messages))]
        hbm = pl.BlockSpec(memory_space=pl.ANY)
        vmem = pl.BlockSpec(memory_space=pltpu.VMEM)
        out = pl.pallas_call(
            functools.partial(body, cfg),
            out_shape=jax.ShapeDtypeStruct((height[3], images, chans[3]), bf16),
            in_specs=[hbm] + [vmem if p in (1, 3) else hbm for _ in range(3) for p in range(5)],
            out_specs=vmem,
            scratch_shapes=scratch,
            compiler_params=pltpu.CompilerParams(collective_id=0, has_side_effects=True, vmem_limit_bytes=60 * 1024 * 1024),
            name="encoder",
        )(x_tile, *operands)
        return jnp.transpose(out, (1, 0, 2))[:, :, None, :]

    return jax.shard_map(local_blocks, mesh=mesh, in_specs=(tile_spec,) + (P(),) * 15, out_specs=tile_spec, check_vma=False)
```

time: 61.6 us -> 56.8 us (0.922)
  Pallas kernels: 59.8 us -> 55.1 us
    pallas_call x1, Pallas kernels: 59.8 us -> 55.1 us  [local_blocks(): pl.pallas_call(functools.partial(body, cfg), out_shape=jax.ShapeDtypeStru...]
where the time goes in v3:
time: 56.8 us; the launch traced here: 56.7 us
  Pallas kernels  55.1 us (97%)
  local copies, waits for them, and re-layouts  1.59 us (3%)
    pallas_call x1, Pallas kernels, local_blocks(): pl.pallas_call(functools.partial(body, cfg), out_shape=jax.ShapeDtypeStru...  55.1 us
    unnamed x1, local copies, waits for them, and re-layouts  1.59 us

profile of v3, /device:TPU:101, one launch (start us, length us, event | category | flops | bytes accessed | tf_op | source)
XLA Modules:
  0.0 56.7 jit_solution(4658673913962267291)
XLA Ops:
  0.0 55.1 %encoder.1 = bf16[12,16,320]{2,1,0:T(8,128)(2,1)} custom-call(bf16[16,96,8,128]{3,2,1,0:T(8,128)(2,1)} %x_hbm.1, bf16[9,128,256]{2,1,0:T(8,128)(2,1)} %bitcast.23, f32[256]{0:T(256)} %refs_1_.1, bf16[9,256,256]{2,1,0:T(8,128)(2,1)} %bitcast.22, f32[256]{0:T(256)} %refs_3_.1, bf16[1,128,256]{2,1,0:T(8,128)(2,1)} %bitcast.27, bf16[9,320,256]{2,1,0:T(8,128)(2,1)} %bitcast.21, ...), custom_call_target="tpu_custom_call" | custom-call | tf_op jit(solution)/shard_map/encoder/pallas_call | solution.py:471
  55.1 1.6 %copy.19 = bf16[16,12,1,320]{3,0,2,1:T(8,128)(2,1)} copy(bf16[16,12,1,320]{3,0,2,1:T(8,128)(2,1)} %bitcast.24) | data formatting | bytes 245760

commit v4 on v3

--- a/solution.py
+++ b/solution.py
@@ -16,12 +16,19 @@
     return -(-channels // LANE)
 
 
-def cut(count, pieces, unit=1):
-    bounds = [round(count * k / pieces / unit) * unit for k in range(pieces + 1)]
-    return [(a, b) for a, b in zip(bounds, bounds[1:]) if b > a]
+def pair(index):
+    return index // 2 + 1, index % 2
+
+
+def cut(count, pieces):
+    bounds = [0] + [(count * k // pieces + 2) // 2 * 2 for k in range(1, pieces)] + [count]
+    return list(zip(bounds, bounds[1:]))
 
 
 WEIGHTS = (0, 2, 4)
+TAPS = range(3)
+LEFT, MIDDLE, RIGHT = (0,), (1,), (2,)
+INNER, LOCAL = LEFT + MIDDLE, MIDDLE + RIGHT
 PACKS = [("y", s, name) for s in range(1, 3) for name in ("left", "right")] + [("z", 2, "left")]
 
 
@@ -96,8 +103,10 @@
 
 def body(cfg, x_hbm, *refs):
     params, refs = refs[:15], refs[15:]
-    out_ref, raw, xs, y1, y2, y3, z1, z2, *ws, packs, load_sems, sems = refs
+    out_ref, raw, xs, y1, y2, y3, z1, z2, *ws, packs, accs, load_sems, sems = refs
     ys, zs = (y1, y2, y3), (z1, z2)
+    w_down, w_conv, w_proj = (list(zip(ws, cfg["transposed"]))[k::3] for k in range(3))
+    b_down, b_conv = (params[k::5] for k in (1, 3))
     chans, height, width = cfg["chans"], cfg["height"], cfg["width"]
     row, col = lax.axis_index("row"), lax.axis_index("col")
     grid = (row, col, cfg["rows"], cfg["cols"])
@@ -106,8 +115,8 @@
     dtype = jnp.bfloat16
     images = cfg["images"]
 
-    xcuts = cut(height[0], cfg["zcut"][0], 2)
-    xloads = [pltpu.make_async_copy(x_hbm.at[:, a:b], raw.at[:, a:b], load_sems.at[9 + k]) for k, (a, b) in enumerate(xcuts)]
+    xcuts = cut(height[1], cfg["pieces"][0])
+    xloads = [pltpu.make_async_copy(x_hbm.at[:, 2 * a:2 * b], raw.at[:, 2 * a:2 * b], load_sems.at[9 + k]) for k, (a, b) in enumerate(xcuts)]
     loads = []
     for stage in range(3):
         for k, p in enumerate(WEIGHTS):
@@ -163,15 +172,23 @@
     def stack(pieces):
         return pieces[0] if len(pieces) == 1 else jnp.concatenate(pieces, axis=0)
 
-    def matrix(ref):
-        value = ref[...]
-        return value.reshape(-1, value.shape[-1])
-
-    def times(lhs, ref, transposed):
+    def times(taps, ref, transposed):
         if transposed:
-            return sum(lax.dot_general(lhs[:, t * ref.shape[2]:(t + 1) * ref.shape[2]], ref[t], (((1,), (1,)), ((), ())), preferred_element_type=jnp.float32)
-                       for t in range(ref.shape[0]))
-        return jnp.dot(lhs, matrix(ref), preferred_element_type=jnp.float32)
+            return sum(lax.dot_general(lhs, ref[t], (((1,), (1,)), ((), ())), preferred_element_type=jnp.float32) for t, lhs in taps)
+        lhs = jnp.concatenate([lhs for _, lhs in taps], axis=1)
+        return jnp.dot(lhs, stack([ref[t] for t, _ in taps]), preferred_element_type=jnp.float32)
+
+    def partial_sum(slot, rows, acc, keep):
+        r = 0
+        parts = []
+        for a, b in rows:
+            n = (b - a) * images
+            if keep == "first":
+                accs[slot, a * images:b * images] = acc[r:r + n]
+            else:
+                parts.append(accs[slot, a * images:b * images])
+            r += n
+        return None if keep == "first" else acc + stack(parts)
 
     def strided(src, ct, runs, kh, kw, c0, nc):
         up, lo = (1 if kh else 0), c0 + (1 if kw else 0)
@@ -181,16 +198,19 @@
         src = zin[s]
         return jnp.concatenate([strided(src, ct, runs, 1, 1, c0, nc) for ct in range(src.shape[0])], axis=1)
 
-    def down(s, rows, c0, nc=1):
+    def down(s, rows, c0, nc=1, kws=TAPS, keep=None):
         src, dst = zin[s], ys[s]
         wait_load(3 * s)
         taps = []
-        for kh in range(3):
-            for kw in range(3):
-                for ct in range(src.shape[0]):
-                    taps.append(strided(src, ct, rows, kh, kw, c0, nc))
-        acc = times(jnp.concatenate(taps, axis=1), ws[3 * s], cfg["transposed"][3 * s])
-        val = jnp.maximum(acc + params[5 * s + 1][...].reshape(1, -1), 0.0).astype(dtype)
+        for kh in TAPS:
+            for kw in kws:
+                taps.append((3 * kh + kw, jnp.concatenate([strided(src, ct, rows, kh, kw, c0, nc) for ct in range(src.shape[0])], axis=1)))
+        acc = times(taps, *w_down[s])
+        if keep:
+            acc = partial_sum(2 * s - 2, rows, acc, keep)
+            if acc is None:
+                return
+        val = jnp.maximum(acc + b_down[s][...].reshape(1, -1), 0.0).astype(dtype)
         n = images * nc
         for ct in range(dst.shape[0]):
             l1 = min(chans[s + 1] - ct * LANE, LANE)
@@ -200,18 +220,22 @@
                 dst[ct, a + 1:b + 1, pl.ds(c0 + 1, nc), :, 0:l1] = part.reshape(b - a, nc, images, l1)
                 r += b - a
 
-    def conv(s, rows, c0, nc=1):
+    def conv(s, rows, c0, nc=1, kws=TAPS, keep=None):
         src = ys[s]
         wait_load(3 * s + 1)
         wait_load(3 * s + 2)
         taps = []
-        for kh in range(3):
-            for kw in range(3):
-                for ct in range(src.shape[0]):
-                    taps.append(stack([flat(src[ct, a + kh:b + kh, pl.ds(c0 + kw, nc)]) for a, b in rows]))
-        acc = times(jnp.concatenate(taps, axis=1), ws[3 * s + 1], cfg["transposed"][3 * s + 1])
-        acc += times(centre(s, rows, c0, nc), ws[3 * s + 2], cfg["transposed"][3 * s + 2])
-        val = jnp.maximum(acc + params[5 * s + 3][...].reshape(1, -1), 0.0).astype(dtype)
+        for kh in TAPS:
+            for kw in kws:
+                taps.append((3 * kh + kw, jnp.concatenate([stack([flat(src[ct, a + kh:b + kh, pl.ds(c0 + kw, nc)]) for a, b in rows]) for ct in range(src.shape[0])], axis=1)))
+        acc = times(taps, *w_conv[s])
+        if keep != "rest":
+            acc += times([(0, centre(s, rows, c0, nc))], *w_proj[s])
+        if keep:
+            acc = partial_sum(2 * s - 1, rows, acc, keep)
+            if acc is None:
+                return
+        val = jnp.maximum(acc + b_conv[s][...].reshape(1, -1), 0.0).astype(dtype)
         n = images * nc
         if s == 2:
             (a, b), = rows
@@ -226,13 +250,13 @@
                 r += b - a
                 even, odd = a + a % 2, b - b % 2
                 for j in range(nc):
-                    into = (lax.div(c0 + j, 2) + 1, lax.rem(c0 + j, 2), slice(None), slice(0, l1))
+                    into = pair(c0 + j) + (slice(None), slice(l1))
                     if a < even:
-                        dst[(ct, a // 2 + 1, 1) + into] = part[0, j]
+                        dst[(ct,) + pair(a) + into] = part[0, j]
                     if odd > even:
                         dst[(ct, slice(even // 2 + 1, odd // 2 + 1), slice(None)) + into] = part[even - a:odd - a, j].reshape((odd - even) // 2, 2, images, l1)
                     if odd < b and b - 1 >= even:
-                        dst[(ct, odd // 2 + 1, 0) + into] = part[b - 1 - a, j]
+                        dst[(ct,) + pair(odd) + into] = part[odd - a, j]
 
     def halves(tile):
         return pltpu.roll(tile.astype(jnp.float32), LANE // 2, tile.ndim - 1).astype(dtype)
@@ -277,17 +301,18 @@
     def send_y_col(s, name, side, k, own, there):
         a, b = ycuts[s][k]
         y = ys[s]
+        rows = slice(1 + a, 1 + b)
         packed = packs_of(("y", s, name), a, b)
-        send_column(exchanges[2 * s + 1], (name, k), side, packed, lambda ct: y.at[ct, 1 + a:1 + b, 1 + own],
-                    lambda ct: y.at[ct, 1 + a:1 + b, 1 + there], y.shape[0] - 1, b - a)
+        send_column(exchanges[2 * s + 1], (name, k), side, packed, lambda ct: y.at[ct, rows, 1 + own],
+                    lambda ct: y.at[ct, rows, 1 + there], y.shape[0] - 1, b - a)
 
     def send_z_col(s, name, side, k, own, there):
         a, b = zcuts[s][k]
         z = zin[s]
         rows = slice(1 + a // 2, 1 + b // 2)
         packed = packs_of(("z", s, name), a, b)
-        send_column(exchanges[2 * s], (name, k), side, packed, lambda ct: z.at[ct, rows, :, (own + 2) // 2, own % 2],
-                    lambda ct: z.at[ct, rows, :, (there + 2) // 2, there % 2], z.shape[0] - 1, b - a)
+        send_column(exchanges[2 * s], (name, k), side, packed, lambda ct: z.at[(ct, rows, slice(None)) + pair(own)],
+                    lambda ct: z.at[(ct, rows, slice(None)) + pair(there)], z.shape[0] - 1, b - a)
 
     def send_y_rows(s, side):
         y, h, w = ys[s], height[s + 1], width[s + 1]
@@ -319,14 +344,14 @@
     def blocks(lo, hi, size):
         return [[(k, min(k + size, hi))] for k in range(lo, hi, size)]
 
-    zcuts = [cut(height[s], cfg["zcut"][s], 2) for s in range(3)]
-    ycuts = [cut(height[s + 1], cfg["ycut"][s], 2) for s in range(3)]
+    ycuts = [cut(height[s + 1], pieces) for s, pieces in enumerate(cfg["pieces"])]
+    zcuts = [[(2 * a, 2 * b) for a, b in cuts] for cuts in ycuts]
 
     def turn(k):
         xloads[k].wait()
         for i in range(*zcuts[0][k]):
             tile = jnp.swapaxes(raw[:, i], 0, 1)
-            xs[0, i // 2 + 1, i % 2, 1:1 + width[0] // 2] = tile.reshape(width[0] // 2, 2, images, LANE)
+            xs[(0,) + pair(i) + (slice(1, None),)] = tile.reshape(width[0] // 2, 2, images, LANE)
 
     turn(0)
     row_inner = jnp.logical_and(row > 0, row + 1 < cfg["rows"])
@@ -378,21 +403,24 @@
     ex.need("row")
     for rows in blocks(0, h2, 12):
         down(1, rows, 1, w2 - 1)
+    down(1, [(0, h2)], 0, kws=LOCAL, keep="first")
     for k, (a, b) in enumerate(ycuts[1]):
         need_z(1, "left", b)
         ex.need("corner")
-        down(1, [(a, b)], 0)
+        down(1, [(a, b)], 0, kws=LEFT, keep="rest")
         send_y_col(1, "right", -1, k, 0, w2)
         send_y_col(1, "left", 1, k, w2 - 1, -1)
         if k == 0:
             send_y_rows(1, -1)
         if b == h2:
             send_y_rows(1, 1)
+    conv(1, [(1, h2 - 1)], 1, kws=INNER, keep="first")
     exchanges[3].need(("row", "r", -1), ("row", "r", 1))
+    conv(1, [(0, 1), (h2 - 1, h2)], 1, kws=INNER, keep="first")
     need_corners(1, "right")
     for k, (a, b) in enumerate(zcuts[2]):
         need_y(1, "right", b)
-        conv(1, [(a, b)], 1, w2 - 1)
+        conv(1, [(a, b)], 1, kws=RIGHT, keep="rest")
         send_z_col(2, "left", 1, k, w2 - 1, -1)
     need_corners(1, "left")
     for k, (a, b) in enumerate(zcuts[2]):
@@ -402,10 +430,11 @@
 
     ex = exchanges[4]
     ex.need("row")
+    down(2, [(0, h3)], 0, kws=LOCAL, keep="first")
     for k, (a, b) in enumerate(ycuts[2]):
         need_z(2, "left", b)
         ex.need("corner")
-        down(2, [(a, b)], 0)
+        down(2, [(a, b)], 0, kws=LEFT, keep="rest")
         send_y_col(2, "right", -1, k, 0, 1)
         send_y_col(2, "left", 1, k, 0, -1)
         if k == 0:
@@ -413,11 +442,12 @@
         if b == h3:
             send_y_rows(2, 1)
     exchanges[5].need(("row", "r", -1), ("row", "r", 1))
+    conv(2, [(0, h3)], 0, kws=MIDDLE, keep="first")
     need_corners(2, "left")
     need_corners(2, "right")
     need_y(2, "left", h3)
     need_y(2, "right", h3)
-    conv(2, [(0, h3)], 0)
+    conv(2, [(0, h3)], 0, kws=LEFT + RIGHT, keep="rest")
     assert counter[0] == sems.shape[1]
     groups = {}
     for ex in exchanges:
@@ -453,9 +483,9 @@
                     wshapes.append((value.shape[0], tiles_of(k) * LANE, n))
                 operands.append(value)
                 transposed.append(flip)
-        zcut, ycut = (4, 3, 3), (4, 3, 2)
-        cfg = dict(chans=chans, height=height, width=width, rows=row_count, cols=col_count, images=images, transposed=transposed, zcut=zcut, ycut=ycut)
-        messages = 65
+        pieces = (4, 4, 2)
+        cfg = dict(chans=chans, height=height, width=width, rows=row_count, cols=col_count, images=images, transposed=transposed, pieces=pieces)
+        messages = 24 + 3 * pieces[0] + 5 * pieces[1] + 6 * pieces[2]
         bf16 = jnp.bfloat16
         scratch = [pltpu.VMEM(x_tile.shape, bf16), pltpu.VMEM((1, tile_h // 2 + 1, 2, tile_w // 2 + 1, 2, images, LANE), bf16)]
         for s in (1, 2, 3):
@@ -465,7 +495,8 @@
         for shape in wshapes:
             scratch.append(pltpu.VMEM(shape, bf16))
         scratch.append(pltpu.VMEM((2, len(PACKS), height[2] // 2, images, LANE), bf16))
-        scratch += [pltpu.SemaphoreType.DMA((9 + zcut[0],)), pltpu.SemaphoreType.DMA((2, messages))]
+        scratch.append(pltpu.VMEM((4, height[2] * images, chans[3]), jnp.float32))
+        scratch += [pltpu.SemaphoreType.DMA((9 + pieces[0],)), pltpu.SemaphoreType.DMA((2, messages))]
         hbm = pl.BlockSpec(memory_space=pl.ANY)
         vmem = pl.BlockSpec(memory_space=pltpu.VMEM)
         out = pl.pallas_call(
@@ -474,7 +505,7 @@
             in_specs=[hbm] + [vmem if p in (1, 3) else hbm for _ in range(3) for p in range(5)],
             out_specs=vmem,
             scratch_shapes=scratch,
-            compiler_params=pltpu.CompilerParams(collective_id=0, has_side_effects=True, vmem_limit_bytes=60 * 1024 * 1024),
+            compiler_params=pltpu.CompilerParams(collective_id=0, has_side_effects=True, vmem_limit_bytes=60 << 20),
             name="encoder",
         )(x_tile, *operands)
         return jnp.transpose(out, (1, 0, 2))[:, :, None, :]

time: 56.8 us -> 55.4 us (0.975)
  Pallas kernels: 55.1 us -> 53.7 us
    pallas_call x1, Pallas kernels: 55.1 us -> 53.7 us  [local_blocks(): pl.pallas_call(functools.partial(body, cfg), out_shape=jax.ShapeDtypeStru...]
where the time goes in v4:
time: 55.4 us; the launch traced here: 55.3 us
  Pallas kernels  53.7 us (97%)
  local copies, waits for them, and re-layouts  1.59 us (3%)
    pallas_call x1, Pallas kernels, local_blocks(): pl.pallas_call(functools.partial(body, cfg), out_shape=jax.ShapeDtypeStru...  53.7 us
    unnamed x1, local copies, waits for them, and re-layouts  1.59 us

profile of v4, /device:TPU:101, one launch (start us, length us, event | category | flops | bytes accessed | tf_op | source)
XLA Modules:
  0.0 55.3 jit_solution(13141782672876314597)
XLA Ops:
  0.0 53.7 %encoder.1 = bf16[12,16,320]{2,1,0:T(8,128)(2,1)} custom-call(bf16[16,96,8,128]{3,2,1,0:T(8,128)(2,1)} %x_hbm.1, bf16[9,128,256]{2,1,0:T(8,128)(2,1)} %bitcast.23, f32[256]{0:T(256)} %refs_1_.1, bf16[9,256,256]{2,1,0:T(8,128)(2,1)} %bitcast.22, f32[256]{0:T(256)} %refs_3_.1, bf16[1,128,256]{2,1,0:T(8,128)(2,1)} %bitcast.27, bf16[9,320,256]{2,1,0:T(8,128)(2,1)} %bitcast.21, ...), custom_call_target="tpu_custom_call" | custom-call | tf_op jit(solution)/shard_map/encoder/pallas_call | solution.py:502
  53.7 1.6 %copy.19 = bf16[16,12,1,320]{3,0,2,1:T(8,128)(2,1)} copy(bf16[16,12,1,320]{3,0,2,1:T(8,128)(2,1)} %bitcast.24) | data formatting | bytes 245760
